TPU v7x, 32 devices: a whole 2x2x4 slice. The times are simulated.
32 devices in a mesh: kv: 16 (over z, y, x), head: 2 (over core).
Axes of the slice: x: 2, y: 2, z: 4, core: 2. Of those that a mesh axis runs over, the one named last changes fastest.
Arguments:
- queries: bfloat16 [8, 256, 128], P('head', 'kv'), may hold values from -384 to 384
- key_cache: bfloat16 [4096, 8, 128, 128], P('kv', 'head'), may hold values from -6 to 6
- value_cache: bfloat16 [4096, 8, 128, 128], P('kv', 'head'), may hold values from -6 to 6
- key_new: bfloat16 [32, 8, 128], P(None, 'head'), may hold values from -6 to 6
- value_new: bfloat16 [32, 8, 128], P(None, 'head'), may hold values from -6 to 6
- lengths: int32 [32], replicated, may hold values from 2 to 16385, as said below
- page_table: int32 [4096], replicated, may hold values from 0 to 4095, each once
Outputs:
- attended: bfloat16 [8, 256, 128], P('head', 'kv')
Inputs may be any that keep to these rules, and one draw needn't show every extreme that they name: The cache holds the first lengths[s] - 1 tokens of sequence s; some sequence has the largest length. `page_table`: every page appears once; page g lies on kv index g // 256.
All inputs are finite; a program needn't handle non-finite values.
Results may differ from a plain program's by a relative error of at most 0.0025.
Values may be sent and summed in bfloat16 or wider, within the bound.
A program may use at most 128 MiB of HBM per device.

v0:
```python
import math

import jax
import jax.numpy as jnp
from jax import lax
from jax.sharding import PartitionSpec as P

LOWEST_SCORE = -1e30


def finish(cache_max, cache_sum, cache_out, query_wide, fresh_key, fresh_value, score_scale):
    new_score = jnp.sum(query_wide * fresh_key.astype(jnp.float32), axis=-1) * score_scale
    highest = jnp.maximum(cache_max, new_score)
    old_part = jnp.exp(cache_max - highest)
    new_part = jnp.exp(new_score - highest)
    numerator = cache_out * old_part[..., None] + new_part[..., None] * fresh_value.astype(
        jnp.float32
    )
    denominator = cache_sum * old_part + new_part
    return (numerator / denominator[..., None]).astype(jnp.bfloat16)


def fold_triples(pieces):
    piece_max, piece_sum, piece_out = pieces
    highest = jnp.max(piece_max, axis=0)
    factor = jnp.exp(piece_max - highest[None])
    return (
        highest,
        jnp.sum(piece_sum * factor, axis=0),
        jnp.sum(piece_out * factor[..., None], axis=0),
    )


def on_device(queries, key_cache, value_cache, key_new, value_new, lengths, page_table):
    all_query = lax.all_gather(queries, "kv", axis=1, tiled=True)
    seq_count = lengths.shape[0]
    page_total = page_table.shape[0]
    pages_here = key_cache.shape[0]
    kv_here = key_cache.shape[1]
    page_len = key_cache.shape[2]
    head_width = key_cache.shape[3]
    rows_all = all_query.shape[1]
    group_size = rows_all // seq_count
    page_slots = page_total // seq_count
    local_rows = queries.shape[1]
    score_scale = 1.0 / math.sqrt(head_width)
    kv_index = lax.axis_index("kv")
    inverse = (
        jnp.zeros((page_total,), jnp.int32)
        .at[page_table]
        .set(jnp.arange(page_total, dtype=jnp.int32))
    )
    local_ids = lax.dynamic_slice_in_dim(inverse, kv_index * pages_here, pages_here)
    page_seq = local_ids // page_slots
    page_slot = local_ids % page_slots
    grouped = all_query.reshape(kv_here, seq_count, group_size, head_width)
    page_query = grouped[:, page_seq]
    scores = (
        jnp.einsum("gpqd,pgtd->pgqt", page_query, key_cache, preferred_element_type=jnp.float32)
        * score_scale
    )
    positions = page_slot[:, None] * page_len + jnp.arange(page_len, dtype=jnp.int32)[None, :]
    in_cache = (positions < (lengths[page_seq] - 1)[:, None])[:, None, None, :]
    masked = jnp.where(in_cache, scores, LOWEST_SCORE)
    page_max = jnp.max(masked, axis=3)
    weights = jnp.where(in_cache, jnp.exp(masked - page_max[..., None]), 0.0)
    page_sum = jnp.sum(weights, axis=3)
    page_out = jnp.einsum(
        "pgqt,pgtd->pgqd",
        weights.astype(jnp.bfloat16),
        value_cache,
        preferred_element_type=jnp.float32,
    )
    member = page_seq[None, :] == jnp.arange(seq_count, dtype=jnp.int32)[:, None]
    seq_best = jnp.max(jnp.where(member[:, :, None, None], page_max[None], LOWEST_SCORE), axis=1)
    factor = jnp.exp(page_max - seq_best[page_seq])
    onehot = member.astype(jnp.float32)
    seq_sum = jnp.einsum("sp,pgq->gsq", onehot, page_sum * factor, precision=lax.Precision.HIGHEST)
    seq_out = jnp.einsum(
        "sp,pgqd->gsqd", onehot, page_out * factor[..., None], precision=lax.Precision.HIGHEST
    )
    seq_max = jnp.transpose(seq_best, (1, 0, 2)).reshape(kv_here, rows_all)
    seq_sum = seq_sum.reshape(kv_here, rows_all)
    seq_out = seq_out.reshape(kv_here, rows_all, head_width)
    cache_max, cache_sum, cache_out = fold_triples(
        (
            lax.all_to_all(seq_max[None], "kv", split_axis=2, concat_axis=0, tiled=True),
            lax.all_to_all(seq_sum[None], "kv", split_axis=2, concat_axis=0, tiled=True),
            lax.all_to_all(seq_out[None], "kv", split_axis=2, concat_axis=0, tiled=True),
        )
    )
    row_seq = (kv_index * local_rows + jnp.arange(local_rows, dtype=jnp.int32)) // group_size
    fresh_key = jnp.transpose(key_new[row_seq], (1, 0, 2))
    fresh_value = jnp.transpose(value_new[row_seq], (1, 0, 2))
    query_wide = queries.astype(jnp.float32)
    return finish(cache_max, cache_sum, cache_out, query_wide, fresh_key, fresh_value, score_scale)


def solution(mesh):
    placed = (
        P("head", "kv", None),
        P("kv", "head", None, None),
        P("kv", "head", None, None),
        P(None, "head", None),
        P(None, "head", None),
        P(),
        P(),
    )
    return jax.shard_map(
        on_device, mesh=mesh, in_specs=placed, out_specs=P("head", "kv", None), check_vma=False
    )
```

profile of v0, /device:TPU:12, one launch (start us, length us, event | category | flops | bytes accessed | tf_op | source)
XLA Modules:
  0.0 172.7 jit_solution(6055094217681499025)
XLA Ops:
  0.0 0.0 copy-start
  0.0 2.1 %fusion.45 = (s32[1]{0:T(128)}, s32[1]{0:T(128)}, s32[1]{0:T(128)}, s32[1]{0:T(128)}, s32[1]{0:T(128)}, /*index=5*/s32[1]{0:T(128)}, s32[1]{0:T(128)}, s32[1]{0:...) fusion(s32[32]{0:T(128)} %param.12), kind=kLoop, calls=%fused_computation.108 | loop fusion | bytes 152 | tf_op jit(solution)/shard_map/gather | solution.py:63
  2.1 1.8 %fusion.46 = (s32[1]{0:T(128)}, s32[1]{0:T(128)}, s32[1]{0:T(128)}, s32[1]{0:T(128)}, s32[1]{0:T(128)}, /*index=5*/s32[1]{0:T(128)}, s32[1]{0:T(128)}, s32[1]{0:...) fusion(s32[32]{0:T(128)} %param.12), kind=kLoop, calls=%fused_computation.109 | loop fusion | bytes 104 | tf_op jit(solution)/shard_map/gather | solution.py:63
  3.9 0.7 compare_select_fusion
  4.7 15.5 %scatter_custom_fusion = s32[4096]{0:T(1024)S(1)} fusion(s32[4096]{0:T(1024)S(1)} %compare_select_fusion, s32[4096]{0:T(1024)S(1)} %iota.23, s32[]{:T(128)} %constant.32.clone.1), kind=kCustom, calls=%fused_computation.48 | custom fusion | bytes 16388 | tf_op jit(solution)/shard_map/scatter | solution.py:51
  20.2 0.1 fusion.35
  20.3 20.1 %fusion.36 = (s32[256]{0:T(256)S(1)}, s32[256]{0:T(256)S(1)}) fusion(s32[]{:T(128)} %bitcast, s32[]{:T(128)} %bitcast.1, s32[]{:T(128)} %bitcast.2, s32[]{:T(128)} %bitcast.3, s32[]{:T(128)} %bitcast.4, s32[]{:T(128)} %bitcast.5, s32[]{:T(128)} %bitcast.6, s32[]{:T(128)} %bitcast.7, s32[]{:T(128)} %bitcast.8, s32[]{:T(128)} %bitcast.9, s32[]{:T(128)} %bitcast.10, ...), kind=kLoop, calls=%fused_computation.100 | loop fusion | flops 20736 | bytes 3204 | tf_op jit(solution)/shard_map/sub | solution.py:63
  40.5 32.5 %all_gather.3 = bf16[4,256,128]{2,1,0:T(8,128)(2,1)S(1)} all-gather(bf16[4,16,128]{2,1,0:T(8,128)(2,1)} %param.7), channel_id=1, replica_groups=mesh['kv'=16,'head'=2] {'kv'}, dimensions={1}, use_global_device_ids=true | all-gather | bytes 278528 | tf_op jit(solution)/shard_map/all_gather | solution.py:35
  73.0 1.3 gather_fusion
  74.3 0.1 add_compare_fusion
  74.5 22.5 %fusion.2 = (f32[256,4,8]{2,1,0:T(4,128)S(1)}, f32[256,4,8,128]{3,2,1,0:T(8,128)}) fusion(pred[256,128]{1,0:T(8,128)(4,1)S(1)} %add_compare_fusion, bf16[256,4,128,128]{3,2,1,0:T(8,128)(2,1)} %param.8, bf16[256,4,8,128]{3,2,1,0:T(8,128)(2,1)S(1)} %gather_fusion), kind=kOutput, calls=%fused_computation.9 | convolution fusion | flops 271572992 | bytes 39911424 | tf_op jit(solution)/shard_map/gpqd,pgtd->pgqt/dot_general | solution.py:59
  97.0 0.2 copy.54
  97.2 0.3 select_reduce_fusion
  97.5 1.0 gather_fusion.1
  98.5 8.4 %fusion.3 = f32[256,4,8]{2,1,0:T(4,128)S(1)} fusion(f32[256,4,8,128]{3,2,1,0:T(8,128)} %get-tuple-element.47, f32[256,4,8]{2,1,0:T(4,128)S(1)} %get-tuple-element.46, pred[256,128]{1,0:T(8,128)(4,1)S(1)} %add_compare_fusion), kind=kLoop, calls=%fused_computation.10 | loop fusion | flops 5234688 | bytes 4292608 | tf_op jit(solution)/shard_map/reduce_sum | solution.py:67
  106.9 0.1 fusion.44
  107.0 0.5 convolution_bitcast_fusion
  107.6 0.8 copy.75
  108.4 13.8 %all-to-all-start.2 = ((f32[1,4,256]{1,0,2:T(1,128)}), f32[1,4,256]{1,0,2:T(1,128)S(1)}, u32[]{:S(2)}, u32[]{:S(2)}) async-start(f32[1,4,256]{1,0,2:T(1,128)} %bitcast.51), calls=%async_computation.2 | async-start | bytes 262144 | tf_op jit(solution)/shard_map/all_to_all | solution.py:88
  122.2 17.7 %broadcast_multiply_fusion = f32[256,4,8,128]{3,2,1,0:T(8,128)} fusion(f32[256,4,8]{2,1,0:T(4,128)S(1)} %bitcast.108, bf16[256,4,128,128]{3,2,1,0:T(8,128)(2,1)} %param.9, f32[256,4,8,128]{3,2,1,0:T(8,128)} %get-tuple-element.47, f32[256,4,8]{2,1,0:T(4,128)S(1)} %get-tuple-element.46, pred[256,128]{1,0:T(8,128)(4,1)S(1)} %add_compare_fusion), kind=kOutput, calls=%fused_computation.15 | convolution fusion | flops 274726912 | bytes 42041344 | tf_op jit(solution)/shard_map/pgqt,pgtd->pgqd/dot_general | solution.py:68
  139.9 0.0 copy-start.1
  139.9 0.0 copy-start.2
  139.9 0.9 copy.74
  140.8 0.0 all-to-all-done.2
  140.8 7.0 %all-to-all-start.1 = ((f32[1,4,256]{1,0,2:T(1,128)}), f32[1,4,256]{1,0,2:T(1,128)S(1)}, u32[]{:S(2)}, u32[]{:S(2)}) async-start(f32[1,4,256]{1,0,2:T(1,128)} %bitcast.42), calls=%async_computation.1 | async-start | bytes 262144 | tf_op jit(solution)/shard_map/all_to_all | solution.py:87
  147.8 5.9 %fusion.16 = f32[4,32,8,128]{3,1,2,0:T(8,128)S(1)} fusion(f32[256,4,8,128]{3,2,1,0:T(8,128)} %broadcast_multiply_fusion, s32[256]{0:T(256)S(1)} %get-tuple-element.13), kind=kOutput, calls=%fused_computation.21 | convolution fusion | flops 402661376 | bytes 4719616 | tf_op jit(solution)/shard_map/sp,pgqd->gsqd/dot_general | solution.py:79
  153.7 0.3 copy.92
  154.0 1.1 copy.57
  155.1 0.0 all-to-all-done.1
  155.1 6.9 %all-to-all-start = ((f32[1,4,256,128]{3,1,0,2:T(4,128)}), f32[1,4,256,128]{3,1,0,2:T(4,128)S(1)}, u32[]{:S(2)}, u32[]{:S(2)}) async-start(f32[1,4,256,128]{3,1,0,2:T(4,128)} %copy.57), calls=%async_computation | async-start | bytes 1048576 | tf_op jit(solution)/shard_map/all_to_all | solution.py:89
  162.1 0.0 copy-done
  162.1 0.6 gather_fusion.2
  162.7 0.0 copy-done.1
  162.7 0.1 fusion.25
  162.8 0.1 copy.63
  162.9 0.0 copy-done.2
  162.9 0.6 gather_fusion.3
  163.5 0.2 copy.70
  163.6 0.2 copy.61
  163.9 0.1 copy.64
  164.0 0.1 copy.66
  164.1 0.1 copy.71
  164.1 7.6 %all-to-all-done = f32[1,4,256,128]{3,1,0,2:T(4,128)S(1)} async-done(((f32[1,4,256,128]{3,1,0,2:T(4,128)}), f32[1,4,256,128]{3,1,0,2:T(4,128)S(1)}, u32[]{:S(2)}, u32[]{:S(2)}) %all-to-all-start) | async-done | bytes 524320 | tf_op jit(solution)/shard_map/all_to_all | solution.py:89
  171.8 0.2 fusion.19
  172.0 0.1 fusion.26
  172.1 0.6 copy.72
  (9 shorter events, 0.1 us)
Async XLA Ops:
  0.0 162.1 %copy-start = (bf16[32,4,128]{2,1,0:T(4,128)(2,1)S(1)}, bf16[32,4,128]{2,1,0:T(4,128)(2,1)}, u32[]{:S(2)}) copy-start(bf16[32,4,128]{2,1,0:T(4,128)(2,1)} %param.10) | copy-start | bytes 98308
  108.4 32.4 %all-to-all-start.2 = ((f32[1,4,256]{1,0,2:T(1,128)}), f32[1,4,256]{1,0,2:T(1,128)S(1)}, u32[]{:S(2)}, u32[]{:S(2)}) async-start(f32[1,4,256]{1,0,2:T(1,128)} %bitcast.51), calls=%async_computation.2 | async-start | bytes 262144 | tf_op jit(solution)/shard_map/all_to_all | solution.py:88
  139.9 22.8 %copy-start.1 = (bf16[4,16,128]{2,1,0:T(8,128)(2,1)S(1)}, bf16[4,16,128]{2,1,0:T(8,128)(2,1)}, u32[]{:S(2)}) copy-start(bf16[4,16,128]{2,1,0:T(8,128)(2,1)} %param.7) | copy-start | bytes 49156
  139.9 22.9 %copy-start.2 = (bf16[32,4,128]{2,1,0:T(4,128)(2,1)S(1)}, bf16[32,4,128]{2,1,0:T(4,128)(2,1)}, u32[]{:S(2)}) copy-start(bf16[32,4,128]{2,1,0:T(4,128)(2,1)} %param.11) | copy-start | bytes 98308
  140.8 14.3 %all-to-all-start.1 = ((f32[1,4,256]{1,0,2:T(1,128)}), f32[1,4,256]{1,0,2:T(1,128)S(1)}, u32[]{:S(2)}, u32[]{:S(2)}) async-start(f32[1,4,256]{1,0,2:T(1,128)} %bitcast.42), calls=%async_computation.1 | async-start | bytes 262144 | tf_op jit(solution)/shard_map/all_to_all | solution.py:87
  155.1 16.6 %all-to-all-start = ((f32[1,4,256,128]{3,1,0,2:T(4,128)}), f32[1,4,256,128]{3,1,0,2:T(4,128)S(1)}, u32[]{:S(2)}, u32[]{:S(2)}) async-start(f32[1,4,256,128]{3,1,0,2:T(4,128)} %copy.57), calls=%async_computation | async-start | bytes 1048576 | tf_op jit(solution)/shard_map/all_to_all | solution.py:89
where the time goes:
time: 176 us; the launch traced here: 173 us
  matrix products  46.7 us (27%)
  blocking collectives  32.5 us (18%)
  other arithmetic  30.5 us (17%)
  starting transfers between devices  27.7 us (16%)
  local copies, waits for them, and re-layouts  27.6 us (16%)
  waiting for transfers between devices  7.64 us (4%)
    all_gather x1, blocking collectives, on_device(): all_query = lax.all_gather(queries, 'kv', axis=1, tiled=True)  32.5 us
    dot_general x1, matrix products, on_device(): jnp.einsum('gpqd,pgtd->pgqt', page_query, key_cache, preferred_element_ty...  22.5 us
    sub x1, other arithmetic, on_device(): in_cache = (positions < (lengths[page_seq] - 1)[:, None])[:, None, None, :]  20.1 us
    dot_general x1, matrix products, on_device(): jnp.einsum('pgqt,pgtd->pgqd', weights.astype(jnp.bfloat16), value_cache,...  17.7 us
    scatter x1, local copies, waits for them, and re-layouts, on_device(): inverse = jnp.zeros((page_total,), jnp.int32).at[page_table].set(jnp.aran...  15.5 us
    all_to_all x1, starting transfers between devices, on_device(): lax.all_to_all(seq_sum[None], 'kv', split_axis=2, concat_axis=0, tiled=True)  13.8 us
    reduce_sum x1, other arithmetic, on_device(): page_sum = jnp.sum(weights, axis=3)  8.45 us
    all_to_all x1, waiting for transfers between devices, on_device(): lax.all_to_all(seq_out[None], 'kv', split_axis=2, concat_axis=0, tiled=True)  7.64 us
  transfers between devices with their start and end apart: 3, of which 1 were waited for; matrix products, arithmetic and copies ran while one was open for 16% of the time, Pallas kernels for 0%

commit v1 on v0

v1 whole, which is shorter than its diff:
```python
import functools
import math

import jax
import jax.numpy as jnp
from jax import lax
from jax.experimental import pallas as pl
from jax.experimental.pallas import tpu as pltpu
from jax.sharding import PartitionSpec as P

LOWEST_SCORE = -1e30
MESH = pl.DeviceIdType.MESH
VMEM = pltpu.VMEM

GROUP = 8
RING = 4

_dot = functools.partial(lax.dot_general, preferred_element_type=jnp.float32)
NT = (((1,), (1,)), ((), ()))
NN = (((1,), (0,)), ((), ()))


def greet(n, me):
    barrier = pltpu.get_barrier_semaphore()
    for k in range(1, n):
        pl.semaphore_signal(
            barrier, inc=1, device_id={"kv": lax.rem(me + k, n)}, device_id_type=MESH
        )
    pl.semaphore_wait(barrier, n - 1)


def gather_kernel(n, x_ref, all_ref, send_sem, recv_sem, own_sem):
    me = lax.axis_index("kv")
    own = pltpu.make_async_copy(x_ref, all_ref.at[me], own_sem)
    own.start()
    greet(n, me)
    copies = []
    for k in range(1, n):
        copy = pltpu.make_async_remote_copy(
            src_ref=x_ref,
            dst_ref=all_ref.at[me],
            send_sem=send_sem.at[k],
            recv_sem=recv_sem.at[me],
            device_id={"kv": lax.rem(me + k, n)},
            device_id_type=MESH,
        )
        copy.start()
        copies.append(copy)
    own.wait()
    for k in range(1, n):
        source = lax.rem(me + k, n)
        pltpu.make_async_remote_copy(
            src_ref=x_ref,
            dst_ref=all_ref.at[source],
            send_sem=send_sem.at[k],
            recv_sem=recv_sem.at[source],
            device_id={"kv": source},
            device_id_type=MESH,
        ).wait_recv()
    for copy in copies:
        copy.wait_send()


def list_kernel(pages_here, page_len, table_ref, length_ref, list_ref):
    me = lax.axis_index("kv")
    seqs, slots = table_ref.shape
    listed = list_ref.shape[1]
    page = table_ref[...] - me * pages_here
    tokens = length_ref[...] - 1 - lax.broadcasted_iota(jnp.int32, (seqs, slots), 1) * page_len
    wanted = (page >= 0) & (page < pages_here) & (tokens > 0)
    flag = jnp.where(wanted, 1.0, 0.0)
    upto = jnp.where(
        lax.broadcasted_iota(jnp.int32, (slots, slots), 0)
        <= lax.broadcasted_iota(jnp.int32, (slots, slots), 1),
        1.0,
        0.0,
    ).astype(jnp.bfloat16)
    inside = _dot(flag.astype(jnp.bfloat16), upto, NN)
    total = jnp.broadcast_to(jnp.sum(flag, axis=1, keepdims=True), (seqs, slots))
    before = jnp.where(
        lax.broadcasted_iota(jnp.int32, (seqs, seqs), 1)
        < lax.broadcasted_iota(jnp.int32, (seqs, seqs), 0),
        1.0,
        0.0,
    ).astype(jnp.bfloat16)
    offset = _dot(before, total.astype(jnp.bfloat16), NN)
    rank = jnp.where(wanted, inside + offset - 1.0, -1.0).astype(jnp.int32)
    wide = jnp.where(wanted, page, 0).astype(jnp.float32)
    held = jnp.where(wanted, jnp.clip(tokens, 0, page_len), 0).astype(jnp.float32)
    row = lax.broadcasted_iota(jnp.int32, (8, slots), 0)
    slot = lax.broadcasted_iota(jnp.int32, (8, slots), 1).astype(jnp.float32)
    place = lax.broadcasted_iota(jnp.int32, (listed, slots), 0)
    out = jnp.zeros((8, listed), jnp.float32)
    for s in range(seqs):
        values = jnp.where(
            row == 0,
            float(s),
            jnp.where(
                row == 1,
                slot,
                jnp.where(
                    row == 2,
                    jnp.broadcast_to(wide[s : s + 1], (8, slots)),
                    jnp.where(row == 3, jnp.broadcast_to(held[s : s + 1], (8, slots)), 0.0),
                ),
            ),
        ).astype(jnp.bfloat16)
        chosen = jnp.where(
            place == jnp.broadcast_to(rank[s : s + 1], (listed, slots)), 1.0, 0.0
        ).astype(jnp.bfloat16)
        out = out + _dot(values, chosen, NT)
    count = jnp.sum(jnp.sum(flag, axis=1, keepdims=True), axis=0, keepdims=True)
    out = jnp.where(
        lax.broadcasted_iota(jnp.int32, (8, listed), 0) == 4,
        jnp.broadcast_to(count, (8, listed)),
        out,
    )
    list_ref[...] = out.astype(jnp.int32)


def attend_kernel(
    group_rows,
    blocks,
    list_ref,
    q_ref,
    keys,
    values,
    out_ref,
    q_wide,
    key_buf,
    value_buf,
    best,
    weight,
    total,
    key_sem,
    value_sem,
):
    heads, page_len, width = key_buf.shape[2:]
    seqs = q_wide.shape[0]
    per_block = seqs // blocks
    scale2 = math.log2(math.e) / math.sqrt(width)
    count = list_ref[4, 0]
    groups = (count + GROUP - 1) // GROUP

    def copies(g, i):
        at = g * GROUP + i
        page = list_ref[2, at]
        slot = lax.rem(g, RING)
        return (
            pltpu.make_async_copy(keys.at[page], key_buf.at[slot, i], key_sem.at[slot, i]),
            pltpu.make_async_copy(values.at[page], value_buf.at[slot, i], value_sem.at[slot, i]),
        )

    def start(g):
        for i in range(GROUP):
            for copy in copies(g, i):
                copy.start()

    for g in range(RING - 1):
        pl.when(g < groups)(functools.partial(start, g))

    best[...] = jnp.full(best.shape, LOWEST_SCORE, jnp.float32)
    weight[...] = jnp.zeros(weight.shape, jnp.float32)
    total[...] = jnp.zeros(total.shape, jnp.float32)
    if q_ref.ndim == 4 and q_ref.shape[2] % group_rows == 0:
        each = q_ref.shape[2] // group_rows
        for d in range(q_ref.shape[0]):
            for h in range(heads):
                block = q_ref[d, h].astype(jnp.float32)
                for j in range(each):
                    q_wide[d * each + j, h] = block[j * group_rows : (j + 1) * group_rows]
    else:
        for d in range(q_ref.shape[0]):
            for h in range(heads):
                rows = q_ref.shape[2]
                parts = group_rows // rows
                q_wide[d // parts, h, (d % parts) * rows : (d % parts + 1) * rows] = q_ref[
                    d, h
                ].astype(jnp.float32)

    lane = lax.broadcasted_iota(jnp.int32, (group_rows, page_len), 1)

    def step(g, carry):
        pl.when(g + RING - 1 < groups)(lambda: start(g + RING - 1))
        slot = lax.rem(g, RING)
        for i in range(GROUP):
            for copy in copies(g, i):
                copy.wait()
        seq = [list_ref[0, g * GROUP + i] for i in range(GROUP)]
        inside = [lane < list_ref[3, g * GROUP + i] for i in range(GROUP)]
        both = [(i, pair) for i in range(GROUP) for pair in range(0, heads, 2)]
        each = [(i, h) for i in range(GROUP) for h in range(heads)]
        scores = {}
        for i, pair in both:
            q2 = q_wide[seq[i], pair : pair + 2].reshape(2 * group_rows, width)
            k2 = key_buf[slot, i, pair : pair + 2].reshape(2 * page_len, width)
            found = _dot(q2.astype(jnp.bfloat16), k2, NT)
            for e in range(2):
                scores[i, pair + e] = found[
                    e * group_rows : (e + 1) * group_rows, e * page_len : (e + 1) * page_len
                ]
        tops, lines = {}, {}
        for i, h in each:
            sc = jnp.where(inside[i], scores[i, h], LOWEST_SCORE)
            scores[i, h] = sc
            tops[i, h] = jnp.broadcast_to(jnp.max(sc, axis=1, keepdims=True), sc.shape)
        for i, h in each:
            lines[i, h] = jnp.where(
                inside[i], jnp.exp2((scores[i, h] - tops[i, h]) * scale2), 0.0
            )
        outs = {}
        for i, pair in both:
            w2 = jnp.concatenate([lines[i, pair], lines[i, pair + 1]], axis=0)
            v2 = jnp.concatenate(
                [value_buf[slot, i, pair], value_buf[slot, i, pair + 1]], axis=1
            )
            found = _dot(w2.astype(jnp.bfloat16), v2, NN)
            for e in range(2):
                outs[i, pair + e] = found[
                    e * group_rows : (e + 1) * group_rows, e * width : (e + 1) * width
                ]
        for i, h in each:
            s = seq[i]
            old = best[s, h]
            new = jnp.maximum(old, tops[i, h])
            keep = jnp.exp2((old - new) * scale2)
            add = jnp.exp2((tops[i, h] - new) * scale2)
            best[s, h] = new
            weight[s, h] = weight[s, h] * keep + lines[i, h] * add
            total[s, h] = total[s, h] * keep + outs[i, h] * add
        return carry

    lax.fori_loop(0, groups, step, 0)

    stat_lane = lax.broadcasted_iota(jnp.int32, (group_rows, width), 1)
    columns = heads * per_block
    for b in range(blocks):
        stats = jnp.zeros((group_rows, width), jnp.float32)
        for j in range(per_block):
            s = b * per_block + j
            for h in range(heads):
                at = h * per_block + j
                out_ref[b, at] = total[s, h]
                mass = jnp.sum(weight[s, h], axis=1, keepdims=True)
                stats = jnp.where(stat_lane == at, best[s, h], stats)
                stats = jnp.where(
                    stat_lane == columns + at, jnp.broadcast_to(mass, stats.shape), stats
                )
        out_ref[b, columns] = stats


def exchange_kernel(
    n, parts, part_ref, q_ref, key_ref, value_ref, out_ref, held, send_sem, recv_sem, own_sem
):
    me = lax.axis_index("kv")
    tiles, group_rows, width = held.shape[1:]
    columns = tiles - 1
    heads = q_ref.shape[0]
    per_block = columns // heads
    own = pltpu.make_async_copy(part_ref.at[me // parts], held.at[me], own_sem)
    own.start()
    greet(n, me)
    copies = []
    for k in range(1, n):
        other = lax.rem(me + k, n)
        copy = pltpu.make_async_remote_copy(
            src_ref=part_ref.at[other // parts],
            dst_ref=held.at[me],
            send_sem=send_sem.at[k],
            recv_sem=recv_sem.at[me],
            device_id={"kv": other},
            device_id_type=MESH,
        )
        copy.start()
        copies.append(copy)
    own.wait()
    for k in range(1, n):
        source = lax.rem(me + k, n)
        pltpu.make_async_remote_copy(
            src_ref=part_ref.at[source // parts],
            dst_ref=held.at[source],
            send_sem=send_sem.at[k],
            recv_sem=recv_sem.at[source],
            device_id={"kv": source},
            device_id_type=MESH,
        ).wait_recv()
    scale = 1.0 / math.sqrt(width)
    scale2 = scale * math.log2(math.e)
    top = held[0, columns]
    for d in range(1, n):
        top = jnp.maximum(top, held[d, columns])
    mass = jnp.zeros_like(top)
    sums = [jnp.zeros_like(top) for _ in range(columns)]
    for d in range(n):
        stats = held[d, columns]
        factor = jnp.exp2((stats - top) * scale2)
        mass = mass + stats * pltpu.roll(factor, columns, 1)
        for c in range(columns):
            sums[c] = sums[c] + held[d, c] * jnp.broadcast_to(factor[:, c : c + 1], top.shape)
    for h in range(heads):
        wide = q_ref[h].astype(jnp.float32)
        results = []
        for j in range(per_block):
            c = h * per_block + j
            s = (me // parts) * per_block + j
            rows = slice(j * group_rows, (j + 1) * group_rows) if parts == 1 else slice(None)
            query = wide[rows]
            shape = query.shape
            fresh_key = jnp.broadcast_to(key_ref[s][h : h + 1].astype(jnp.float32), shape)
            fresh_value = jnp.broadcast_to(value_ref[s][h : h + 1].astype(jnp.float32), shape)
            new = jnp.broadcast_to(jnp.sum(query * fresh_key, axis=1, keepdims=True), shape)

            def mine(x):
                if parts == 1:
                    return x
                size = group_rows // parts
                picked = x[:size]
                for p in range(1, parts):
                    picked = jnp.where(
                        lax.rem(me, parts) == p, x[p * size : (p + 1) * size], picked
                    )
                return picked

            old = mine(jnp.broadcast_to(top[:, c : c + 1], top.shape))
            old_mass = mine(jnp.broadcast_to(mass[:, columns + c : columns + c + 1], top.shape))
            old_sum = mine(sums[c])
            highest = jnp.maximum(old, new)
            old_part = jnp.exp2((old - highest) * scale2)
            new_part = jnp.exp2((new - highest) * scale2)
            results.append(
                (old_sum * old_part + new_part * fresh_value) / (old_mass * old_part + new_part)
            )
        out_ref[h] = jnp.concatenate(results, axis=0).astype(out_ref.dtype)
    for copy in copies:
        copy.wait_send()


def on_device(n, queries, key_cache, value_cache, key_new, value_new, lengths, page_table):
    heads, local_rows, width = queries.shape
    seqs = lengths.shape[0]
    slots = page_table.shape[0] // seqs
    pages_here, _, page_len, _ = key_cache.shape
    group_rows = local_rows * n // seqs
    parts = max(1, group_rows // local_rows)
    blocks = n // parts
    tiles = heads * (seqs // blocks) + 1
    listed = -(-pages_here // 128) * 128 + 128
    vmem = pl.BlockSpec(memory_space=VMEM)
    smem = pl.BlockSpec(memory_space=pltpu.SMEM)
    hbm = pl.BlockSpec(memory_space=pl.ANY)

    pages = pl.pallas_call(
        functools.partial(list_kernel, pages_here, page_len),
        out_shape=jax.ShapeDtypeStruct((8, listed), jnp.int32),
        in_specs=[vmem] * 2,
        out_specs=vmem,
        name="pages_in_cache",
    )(page_table.reshape(seqs, slots), lengths.reshape(seqs, 1))

    every_query = pl.pallas_call(
        functools.partial(gather_kernel, n),
        out_shape=jax.ShapeDtypeStruct((n,) + queries.shape, queries.dtype),
        in_specs=[vmem],
        out_specs=vmem,
        scratch_shapes=[
            pltpu.SemaphoreType.DMA((n,)),
            pltpu.SemaphoreType.DMA((n,)),
            pltpu.SemaphoreType.DMA,
        ],
        compiler_params=pltpu.CompilerParams(collective_id=0, has_side_effects=True),
        name="gather_queries",
    )(queries)

    part = pl.pallas_call(
        functools.partial(attend_kernel, group_rows, blocks),
        out_shape=jax.ShapeDtypeStruct((blocks, tiles, group_rows, width), jnp.float32),
        in_specs=[smem, vmem, hbm, hbm],
        out_specs=vmem,
        scratch_shapes=[
            VMEM((seqs, heads, group_rows, width), jnp.float32),
            VMEM((RING, GROUP, heads, page_len, width), key_cache.dtype),
            VMEM((RING, GROUP, heads, page_len, width), value_cache.dtype),
            VMEM((seqs, heads, group_rows, page_len), jnp.float32),
            VMEM((seqs, heads, group_rows, page_len), jnp.float32),
            VMEM((seqs, heads, group_rows, width), jnp.float32),
            pltpu.SemaphoreType.DMA((RING, GROUP)),
            pltpu.SemaphoreType.DMA((RING, GROUP)),
        ],
        compiler_params=pltpu.CompilerParams(vmem_limit_bytes=48 * 1024 * 1024),
        name="attend_pages",
    )(pages, every_query, key_cache, value_cache)

    return pl.pallas_call(
        functools.partial(exchange_kernel, n, parts),
        out_shape=jax.ShapeDtypeStruct(queries.shape, jnp.bfloat16),
        in_specs=[vmem] * 4,
        out_specs=vmem,
        scratch_shapes=[
            VMEM((n, tiles, group_rows, width), jnp.float32),
            pltpu.SemaphoreType.DMA((n,)),
            pltpu.SemaphoreType.DMA((n,)),
            pltpu.SemaphoreType.DMA,
        ],
        compiler_params=pltpu.CompilerParams(collective_id=1, has_side_effects=True),
        name="exchange_and_finish",
    )(part, queries, key_new, value_new)


def solution(mesh):
    placed = (
        P("head", "kv", None),
        P("kv", "head", None, None),
        P("kv", "head", None, None),
        P(None, "head", None),
        P(None, "head", None),
        P(),
        P(),
    )
    return jax.shard_map(
        functools.partial(on_device, mesh.shape["kv"]),
        mesh=mesh,
        in_specs=placed,
        out_specs=P("head", "kv", None),
        check_vma=False,
    )
```

time: 176 us -> 55.2 us (0.31); the launches traced: 173 us -> 54.4 us
  Pallas kernels: 0 us -> 49.2 us
  matrix products: 46.7 us -> 0 us
  blocking collectives: 32.5 us -> 0 us
  other arithmetic: 30.5 us -> 0 us
  starting transfers between devices: 27.7 us -> 0 us
  local copies, waits for them, and re-layouts: 27.6 us -> 5.12 us
  waiting for transfers between devices: 7.64 us -> 0 us
    pallas_call x0 -> x4, Pallas kernels: none -> 49.2 us  [the longest x1 20.4 us: on_device(): pl.pallas_call(functools.partial(exchange_kernel, n, parts), out_shape=ja...]
    dot_general x4 -> x0, matrix products: 46.7 us -> none  [the longest x1 22.5 us: on_device(): jnp.einsum('gpqd,pgtd->pgqt', page_query, key_cache, preferred_element_ty...]
    all_gather x1 -> x0, blocking collectives: 32.5 us -> none  [on_device(): all_query = lax.all_gather(queries, 'kv', axis=1, tiled=True)]
    all_to_all x3 -> x0, starting transfers between devices: 27.7 us -> none  [the longest x1 13.8 us: on_device(): lax.all_to_all(seq_sum[None], 'kv', split_axis=2, concat_axis=0, tiled=True)]
    sub x1 -> x0, other arithmetic: 20.1 us -> none  [on_device(): in_cache = (positions < (lengths[page_seq] - 1)[:, None])[:, None, None, :]]
    scatter x1 -> x0, local copies, waits for them, and re-layouts: 15.5 us -> none  [on_device(): inverse = jnp.zeros((page_total,), jnp.int32).at[page_table].set(jnp.aran...]
    reduce_sum x4 -> x0, other arithmetic: 8.78 us -> none  [the longest x1 8.45 us: on_device(): page_sum = jnp.sum(weights, axis=3)]
    all_to_all x3 -> x0, waiting for transfers between devices: 7.64 us -> none  [the longest x1 7.64 us: on_device(): lax.all_to_all(seq_out[None], 'kv', split_axis=2, concat_axis=0, tiled=True)]
  transfers between devices with their start and end apart: 3 -> 0, of which waited for: 1 -> 0; matrix products, arithmetic and copies ran while one was open for 16% -> 0% of each run, Pallas kernels for 0% -> 0%
where the time goes in v1:
time: 55.2 us; the launch traced here: 54.4 us
  Pallas kernels  49.2 us (89%)
  local copies, waits for them, and re-layouts  5.12 us (9%)
    pallas_call x1, Pallas kernels, on_device(): pl.pallas_call(functools.partial(exchange_kernel, n, parts), out_shape=ja...  20.4 us
    pallas_call x1, Pallas kernels, on_device(): pl.pallas_call(functools.partial(attend_kernel, group_rows, blocks), out_...  13.4 us
    pallas_call x1, Pallas kernels, on_device(): pl.pallas_call(functools.partial(gather_kernel, n), out_shape=jax.ShapeDt...  12.6 us
    unnamed x7, local copies, waits for them, and re-layouts  3.78 us
    pallas_call x1, Pallas kernels, on_device(): pl.pallas_call(functools.partial(list_kernel, pages_here, page_len), out_...  2.8 us
    reshape x1, local copies, waits for them, and re-layouts, on_device(): lengths.reshape(seqs, 1)  1.34 us

profile of v1, /device:TPU:12, one launch (start us, length us, event | category | flops | bytes accessed | tf_op | source)
XLA Modules:
  0.0 54.4 jit_solution(14419086949316290794)
XLA Ops:
  0.0 1.3 %copy.8.length_ref = s32[32,1]{1,0:T(8,128)} copy(s32[32,1]{0,1:T(1,128)} %bitcast.3) | data formatting | bytes 256 | tf_op jit(solution)/shard_map/reshape | solution.py:358
  1.3 2.8 %pages_in_cache.1.list_ref = s32[8,384]{1,0:T(8,128)} custom-call(s32[32,128]{1,0:T(8,128)} %bitcast.2, s32[32,1]{1,0:T(8,128)} %copy.8.length_ref), custom_call_target="tpu_custom_call" | custom-call | tf_op jit(solution)/shard_map/pages_in_cache/pallas_call | solution.py:352
  4.1 12.6 %gather_queries.1.q_ref = bf16[16,4,16,128]{3,2,1,0:T(8,128)(2,1)} custom-call(bf16[4,16,128]{2,1,0:T(8,128)(2,1)} %q_ref.1), custom_call_target="tpu_custom_call" | custom-call | tf_op jit(solution)/shard_map/gather_queries/pallas_call | solution.py:360
  16.8 0.0 copy-start.1
  16.8 0.9 %copy-done.1 = bf16[16,4,16,128]{3,2,1,0:T(8,128)(2,1)S(1)} copy-done((bf16[16,4,16,128]{3,2,1,0:T(8,128)(2,1)S(1)}, bf16[16,4,16,128]{3,2,1,0:T(8,128)(2,1)}, u32[]{:S(2)}) %copy-start.1) | copy-done | bytes 262168
  17.7 0.0 copy-start.2
  17.7 0.7 %copy-done.2 = s32[8,384]{1,0:T(8,128)S(1)} copy-done((s32[8,384]{1,0:T(8,128)S(1)}, s32[8,384]{1,0:T(8,128)}, u32[]{:S(2)}) %copy-start.2) | copy-done | bytes 12312
  18.4 13.4 %attend_pages.1.part_ref = f32[16,9,8,128]{3,2,1,0:T(8,128)S(1)} custom-call(s32[8,384]{1,0:T(8,128)S(1)} %copy-done.2, bf16[16,4,16,128]{3,2,1,0:T(8,128)(2,1)S(1)} %copy-done.1, bf16[256,4,128,128]{3,2,1,0:T(8,128)(2,1)} %keys.1, bf16[256,4,128,128]{3,2,1,0:T(8,128)(2,1)} %values.1), custom_call_target="tpu_custom_call" | custom-call | tf_op jit(solution)/shard_map/attend_pages/pallas_call | solution.py:374
  31.8 0.0 copy-start
  31.9 0.8 %copy-done = f32[16,9,8,128]{3,2,1,0:T(8,128)} copy-done((f32[16,9,8,128]{3,2,1,0:T(8,128)}, f32[16,9,8,128]{3,2,1,0:T(8,128)S(1)}, u32[]{:S(2)}) %copy-start) | copy-done | bytes 589848
  32.7 20.4 %exchange_and_finish.1 = bf16[4,16,128]{2,1,0:T(8,128)(2,1)} custom-call(f32[16,9,8,128]{3,2,1,0:T(8,128)} %copy-done, bf16[4,16,128]{2,1,0:T(8,128)(2,1)} %q_ref.1, bf16[32,4,128]{2,1,0:T(4,128)(2,1)} %key_ref.1, bf16[32,4,128]{2,1,0:T(4,128)(2,1)} %value_ref.1), custom_call_target="tpu_custom_call" | custom-call | tf_op jit(solution)/shard_map/exchange_and_finish/pallas_call | solution.py:393
  53.0 1.3 %copy.10 = bf16[4,16,128]{2,1,0:T(8,128)(2,1)} copy(bf16[4,16,128]{2,1,0:T(8,128)(2,1)} %exchange_and_finish.1) | data formatting | bytes 32768
Async XLA Ops:
  16.8 1.0 %copy-start.1 = (bf16[16,4,16,128]{3,2,1,0:T(8,128)(2,1)S(1)}, bf16[16,4,16,128]{3,2,1,0:T(8,128)(2,1)}, u32[]{:S(2)}) copy-start(bf16[16,4,16,128]{3,2,1,0:T(8,128)(2,1)} %gather_queries.1.q_ref) | copy-start | bytes 786436
  17.7 0.7 %copy-start.2 = (s32[8,384]{1,0:T(8,128)S(1)}, s32[8,384]{1,0:T(8,128)}, u32[]{:S(2)}) copy-start(s32[8,384]{1,0:T(8,128)} %pages_in_cache.1.list_ref) | copy-start | bytes 36868
  31.8 0.8 %copy-start = (f32[16,9,8,128]{3,2,1,0:T(8,128)}, f32[16,9,8,128]{3,2,1,0:T(8,128)S(1)}, u32[]{:S(2)}) copy-start(f32[16,9,8,128]{3,2,1,0:T(8,128)S(1)} %attend_pages.1.part_ref) | copy-start | bytes 1769476
